TPU v7x, 256 devices: a 8x8x2 block of a 8x8x16 slice. The times are simulated.
256 devices in a mesh: grp: 2 (over z), row: 16 (over x, core), sub: 8 (over y).
Axes of the slice: x: 8, y: 8, z: 2, core: 2. Of those that a mesh axis runs over, the one named last changes fastest.
The devices are a block of a 8x8x16 slice.
Arguments:
- residual_in: float32 [4, 2048, 2048], P('grp', ('row', 'sub')), parts along dimension 0, may hold values from -100 to 100
- direction: float32 [4, 2048, 2048], P('grp', ('row', 'sub')), parts along dimension 0, may hold values from -100 to 100
- spectrum: float32 [8192, 4096], P('grp', ('row', 'sub')), parts along dimension 0, may hold values from 0.0999 to 10.001, as said below
- noise_var: float32 [2], P('grp'), parts along dimension 0, may hold values from 0.5 to 2
Outputs:
- residual_out: float32 [4, 2048, 2048], P('grp', ('row', 'sub')), parts along dimension 0
- direction_out: float32 [4, 2048, 2048], P('grp', ('row', 'sub')), parts along dimension 0
- step_size: float32 [4], P('grp'), parts along dimension 0
There are 2 independent parts, one for each index of `grp`. A program takes and returns all parts, laid end to end along the dimension named above; each array names one. Nothing has to cross between parts.
Inputs may be any that keep to these rules, and one draw needn't show every extreme that they name: spectrum[k, l] = spectrum[(4096 - k) % 4096, (4096 - l) % 4096] for all k, l.
All inputs are finite; a program needn't handle non-finite values.
Results may differ from a plain program's by a relative error of at most 0.00005.
Values sent between devices are 32-bit elements; how exact they have to be, the bound alone decides.
A program may use at most 64 MiB of HBM per device.

v0:
```python
import functools
import math
import jax
import jax.numpy as jnp
from jax import lax
from jax.sharding import Mesh
from jax.sharding import PartitionSpec as P

ROW = ("row_0", "row_1")
ROW_SUB = ("row_0", "row_1", "sub")
high_factor = 128
tiny_value = 1e-06


def split_up(value, dim, count):
    dims = value.shape
    parts = value.reshape(*dims[:dim], count, dims[dim] // count, *dims[dim + 1 :])
    return jnp.moveaxis(parts, dim, 0)


def edges_of(length, count):
    hop = length // count
    if hop >= 8:
        hop -= hop % 8
    return [hop * k for k in range(1, count)]


def laid_out(parts, dim):
    dims = list(parts.shape[1:])
    dims[dim] *= parts.shape[0]
    return jnp.moveaxis(parts, 0, dim).reshape(dims)


def exchange_in_pieces(value, axis, pieces, split_dim, concat_dim):
    parts = split_up(value, split_dim, lax.axis_size(axis))
    cut = max(range(1, max(2, parts.ndim - 1)), key=lambda d: parts.shape[d])
    finished = []
    for share in jnp.split(parts, edges_of(parts.shape[cut], pieces), axis=cut):
        if share.size:
            finished.append(lax.all_to_all(share, axis, split_axis=0, concat_axis=0, tiled=True))
    return laid_out(jnp.concatenate(finished, axis=cut), concat_dim)


def over_axes(value, axes):
    return functools.reduce(lax.psum, axes, value)


def phase_pair(left_ids, right_ids, modulus, orient):
    turns = left_ids * right_ids % modulus
    angle = orient * 2.0 * math.pi / modulus * turns.astype(jnp.float32)
    return (jnp.cos(angle), jnp.sin(angle))


def complex_table(cos_part, sin_part):
    upper_rows = jnp.stack([cos_part, sin_part], axis=1)
    lower_rows = jnp.stack([-sin_part, cos_part], axis=1)
    return jnp.stack([upper_rows, lower_rows], axis=1)


def rotate(values, cos_part, sin_part, at_axis):
    real_part = lax.index_in_dim(values, 0, at_axis, keepdims=False)
    imag_part = lax.index_in_dim(values, 1, at_axis, keepdims=False)
    return jnp.stack(
        [real_part * cos_part - imag_part * sin_part, real_part * sin_part + imag_part * cos_part],
        axis=at_axis,
    )


def contract(form_spec, operand, table_arr):
    return jnp.einsum(form_spec, operand, table_arr, precision=lax.Precision.HIGHEST)


def body(residual_in, direction, spectrum, noise_var):
    probes, rows_dev, grid_len = direction.shape
    embed_len = 2 * grid_len
    low_factor = embed_len // high_factor
    half_factor = grid_len // high_factor
    n_row = lax.axis_size(ROW)
    n_sub = lax.axis_size("sub")
    devices = n_row * n_sub
    per_device = high_factor // devices
    slot_ids = jnp.arange(high_factor, dtype=jnp.int32)
    first_ids = jnp.arange(half_factor, dtype=jnp.int32)
    second_ids = jnp.arange(low_factor, dtype=jnp.int32)
    short_cos, short_sin = phase_pair(first_ids[:, None], second_ids[None, :], low_factor, -1.0)
    turn_cos, turn_sin = phase_pair(slot_ids[:, None], second_ids[None, :], embed_len, -1.0)
    long_cos, long_sin = phase_pair(slot_ids[:, None], slot_ids[None, :], high_factor, -1.0)
    plain_cos, plain_sin = phase_pair(slot_ids[:, None], slot_ids[None, :], high_factor, -1.0)
    back_cos, back_sin = phase_pair(slot_ids[:, None], slot_ids[None, :], high_factor, 1.0)
    perm_cos, perm_sin = phase_pair(slot_ids[:, None], slot_ids[None, :], high_factor, 1.0)
    last_cos, last_sin = phase_pair(second_ids[:, None], first_ids[None, :], low_factor, 1.0)
    fields = direction.reshape(probes // 2, 2, rows_dev, half_factor, high_factor)
    spread = contract("ycrab,acdm->yrbdm", fields, complex_table(short_cos, short_sin))
    batches = spread.shape[0]
    spread = rotate(spread, turn_cos, turn_sin, 3)
    row_freq = contract("frbcm,bcdk->frkdm", spread, complex_table(long_cos, long_sin))
    row_freq = row_freq.reshape(batches, rows_dev, 2 * embed_len)
    columns = exchange_in_pieces(row_freq, ROW_SUB, 2, 2, 1)
    columns = columns.reshape(batches, half_factor, high_factor, per_device, 2, low_factor)
    turned = contract("fabqcm,acdj->fjbqdm", columns, complex_table(short_cos, short_sin))
    turned = rotate(turned, turn_cos.T[:, :, None, None], turn_sin.T[:, :, None, None], 4)
    spectra = contract("fjbqcm,bcdk->fkjqdm", turned, complex_table(plain_cos, plain_sin))
    weights = (spectrum * (1.0 / (embed_len * embed_len))).reshape(
        high_factor, low_factor, per_device, low_factor
    )
    spectra = spectra * weights[None, :, :, :, None, :]
    inverted = contract("fkjqcm,kcdb->fbjqdm", spectra, complex_table(back_cos, back_sin))
    inverted = rotate(inverted, turn_cos[:, :, None, None], -turn_sin[:, :, None, None], 4)
    grid_cols = contract("fbjqcm,jcda->fabqdm", inverted, complex_table(last_cos, last_sin))
    grid_cols = grid_cols.reshape(batches, grid_len, 2 * embed_len // devices)
    rows_back = lax.all_to_all(grid_cols, ROW_SUB, split_axis=1, concat_axis=2, tiled=True)
    rows_back = rows_back.reshape(batches, rows_dev, high_factor, 2, low_factor)
    mixed = contract("frkcm,kcdb->frbdm", rows_back, complex_table(perm_cos, perm_sin))
    mixed = rotate(mixed, turn_cos, -turn_sin, 3)
    applied = contract("frbcm,mcda->fdrab", mixed, complex_table(last_cos, last_sin))
    applied = applied.reshape(probes, rows_dev, grid_len)
    image_out = applied + noise_var[0] * direction
    own_curv = jnp.sum(direction * image_out, axis=(1, 2))
    own_norm = jnp.sum(residual_in * residual_in, axis=(1, 2))
    old_norm, curvature = (over_axes(own_norm, ROW_SUB), over_axes(own_curv, ROW_SUB))
    step_size = old_norm / curvature
    residual_out = residual_in - step_size[:, None, None] * image_out
    new_norm = over_axes(jnp.sum(residual_out * residual_out, axis=(1, 2)), ROW_SUB)
    direction_out = residual_out + (new_norm / (old_norm + tiny_value))[:, None, None] * direction
    return (residual_out, direction_out, step_size)


def solution(mesh):
    torus = Mesh(
        mesh.devices.reshape(mesh.shape["grp"], 8, 2, mesh.shape["sub"]),
        ("grp", "row_0", "row_1", "sub"),
    )
    in_specs = (P("grp", ROW_SUB, None), P("grp", ROW_SUB, None), P("grp", ROW_SUB), P("grp"))
    out_specs = (P("grp", ROW_SUB, None), P("grp", ROW_SUB, None), P("grp"))
    return jax.shard_map(body, mesh=torus, in_specs=in_specs, out_specs=out_specs, check_vma=False)
```

profile of v0, /device:TPU:514, one launch (start us, length us, event | category | flops | bytes accessed | tf_op | source)
XLA Modules:
  0.0 187.7 jit_solution(11520293836639985032)
XLA Ops:
  0.8 0.1 fusion.44
  0.8 0.3 multiply_sine_fusion
  1.1 0.3 fusion.23
  1.4 1.0 copy.72
  2.4 0.6 convolution_bitcast_fusion.5
  3.1 0.1 multiply_subtract_fusion.4
  3.2 0.6 convolution_bitcast_fusion.4
  3.9 0.2 copy.44
  4.1 1.0 reshape.538
  5.2 26.7 %all-to-all-start.1 = ((f32[128,1,512]{2,1,0:T(1,128)}), f32[128,1,512]{2,1,0:T(1,128)S(1)}, u32[]{:S(2)}, u32[]{:S(2)}) async-start(f32[128,1,512]{2,1,0:T(1,128)} %reshape.538), calls=%async_computation.1 | async-start | bytes 524288 | tf_op jit(solution)/shard_map/all_to_all | solution.py:40
  31.9 0.2 copy.43
  32.2 1.0 reshape.540
  33.2 0.7 mul.760
  33.9 1.5 copy.47
  35.4 0.7 fusion.52
  36.1 0.7 fusion.42
  36.8 8.1 %all-to-all-done.1 = f32[128,1,512]{2,1,0:T(1,128)S(1)} async-done(((f32[128,1,512]{2,1,0:T(1,128)}), f32[128,1,512]{2,1,0:T(1,128)S(1)}, u32[]{:S(2)}, u32[]{:S(2)}) %all-to-all-start.1) | async-done | bytes 262176 | tf_op jit(solution)/shard_map/all_to_all | solution.py:40
  44.9 8.5 %all-to-all-start = ((f32[128,1,512]{2,1,0:T(1,128)}), f32[128,1,512]{2,1,0:T(1,128)S(1)}, u32[]{:S(2)}, u32[]{:S(2)}) async-start(f32[128,1,512]{2,1,0:T(1,128)} %reshape.540), calls=%async_computation | async-start | bytes 524288 | tf_op jit(solution)/shard_map/all_to_all | solution.py:40
  53.4 0.1 fusion.57
  53.5 0.6 maximum_bitcast_fusion.18
  54.1 0.3 fusion.22
  54.4 0.3 multiply_sine_fusion.1
  54.6 0.7 maximum_bitcast_fusion.8
  55.3 0.5 broadcast.730
  55.8 1.3 reduce
  57.1 0.1 reshape.539
  57.2 9.2 %all-to-all-done = f32[128,1,512]{2,1,0:T(1,128)S(1)} async-done(((f32[128,1,512]{2,1,0:T(1,128)}), f32[128,1,512]{2,1,0:T(1,128)S(1)}, u32[]{:S(2)}, u32[]{:S(2)}) %all-to-all-start) | async-done | bytes 262176 | tf_op jit(solution)/shard_map/all_to_all | solution.py:40
  66.5 1.3 reduce.1
  67.7 0.1 reshape.541
  67.9 0.1 pad_maximum_fusion
  68.0 1.2 reshape.509
  69.2 0.9 copy.45
  70.1 1.0 convolution_bitcast_fusion
  71.1 0.2 multiply_subtract_fusion.1
  71.3 0.1 maximum_bitcast_fusion
  71.4 0.8 copy-done.1
  72.1 1.7 fusion.1
  73.9 1.0 convolution_bitcast_fusion.1
  74.9 0.2 multiply_subtract_fusion
  75.1 0.1 maximum_bitcast_fusion.1
  75.1 0.4 copy-done.7
  75.6 1.2 convolution_bitcast_fusion.6
  76.8 0.1 reshape.513
  76.9 0.6 copy.51
  77.6 9.6 %reduce.2 = f32[2048,64]{1,0:T(8,128)S(1)} reduce(f32[2048,1,64]{2,1,0:T(1,128)S(1)} %bitcast.174, f32[]{:T(128)} %broadcast.730), dimensions={1}, to_apply=%bitcast.155.reduce_sub_computation | reduce | bytes 1048580
  87.2 1.4 reshape.542
  88.6 8.4 %all-to-all-start.2 = ((f32[128,1,1024]{2,1,0:T(1,128)}), f32[128,1,1024]{2,1,0:T(1,128)S(1)}, u32[]{:S(2)}, u32[]{:S(2)}) async-start(f32[128,1,1024]{2,1,0:T(1,128)} %reshape.542), calls=%async_computation.2 | async-start | bytes 1048576 | tf_op jit(solution)/shard_map/all_to_all | solution.py:111
  97.7 0.1 multiply_reduce_fusion.2
  97.8 17.1 %all-to-all-done.2 = f32[128,1,1024]{2,1,0:T(1,128)S(1)} async-done(((f32[128,1,1024]{2,1,0:T(1,128)}), f32[128,1,1024]{2,1,0:T(1,128)S(1)}, u32[]{:S(2)}, u32[]{:S(2)}) %all-to-all-start.2) | async-done | bytes 524320 | tf_op jit(solution)/shard_map/all_to_all | solution.py:111
  114.9 1.9 %reduce.3 = f32[128,1024]{1,0:T(8,128)S(1)} reduce(f32[128,1,1024]{2,1,0:T(1,128)S(1)} %all-to-all-done.2, f32[]{:T(128)} %broadcast.730), dimensions={1}, to_apply=%all_to_all.19.reduce_sub_computation | reduce | bytes 1048580 | tf_op jit(solution)/shard_map/all_to_all | solution.py:111
  116.8 1.3 reshape.543
  118.1 0.4 copy.52
  118.6 0.6 convolution_bitcast_fusion.3
  119.2 0.1 multiply_subtract_fusion.3
  119.2 0.4 convolution_bitcast_fusion.7
  119.7 0.1 multiply_reduce_fusion.1
  119.9 15.7 %all-reduce.1 = (f32[2]{0:T(128)S(1)}, f32[2]{0:T(128)S(1)}) all-reduce(f32[2]{0:T(128)S(1)} %multiply_reduce_fusion.2, f32[2]{0:T(128)S(1)} %multiply_reduce_fusion.1), channel_id=1, replica_groups=mesh['grp'=2,'row_0'=8,'row_1'=2,'sub'=8] {'row_0'}, use_global_device_ids=true, to_apply=%region_1.2 | all-reduce | flops 4 | bytes 32 | tf_op jit(solution)/shard_map/psum | solution.py:45
  135.6 2.5 %all-reduce.2 = (f32[2]{0:T(128)S(1)}, f32[2]{0:T(128)S(1)}) all-reduce(f32[2]{0:T(128)S(1)} %get-tuple-element.5, f32[2]{0:T(128)S(1)} %get-tuple-element.6), channel_id=1, replica_groups=mesh['grp'=2,'row_0'=8,'row_1'=2,'sub'=8] {'row_1'}, use_global_device_ids=true, to_apply=%region_2.3 | all-reduce | flops 4 | bytes 32 | tf_op jit(solution)/shard_map/psum | solution.py:45
  138.1 16.5 %all-reduce = (f32[2]{0:T(128)S(1)}, f32[2]{0:T(128)S(1)}) all-reduce(f32[2]{0:T(128)S(1)} %get-tuple-element.7, f32[2]{0:T(128)S(1)} %get-tuple-element.8), channel_id=1, replica_groups=mesh['grp'=2,'row_0'=8,'row_1'=2,'sub'=8] {'sub'}, use_global_device_ids=true, to_apply=%region_3.4 | all-reduce | flops 4 | bytes 32 | tf_op jit(solution)/shard_map/psum | solution.py:45
  154.7 0.2 multiply_reduce_fusion
  154.9 15.3 %psum.69 = f32[2]{0:T(128)S(1)} all-reduce(f32[2]{0:T(128)S(1)} %get-tuple-element.9), channel_id=1, replica_groups=mesh['grp'=2,'row_0'=8,'row_1'=2,'sub'=8] {'row_0'}, use_global_device_ids=true, to_apply=%region_9.10 | all-reduce | flops 2 | bytes 16 | tf_op jit(solution)/shard_map/psum | solution.py:45
  170.2 2.5 %psum.70 = f32[2]{0:T(128)S(1)} all-reduce(f32[2]{0:T(128)S(1)} %psum.69), channel_id=1, replica_groups=mesh['grp'=2,'row_0'=8,'row_1'=2,'sub'=8] {'row_1'}, use_global_device_ids=true, to_apply=%region_10.11 | all-reduce | flops 2 | bytes 16 | tf_op jit(solution)/shard_map/psum | solution.py:45
  172.7 14.2 %psum.71 = f32[2]{0:T(128)S(1)} all-reduce(f32[2]{0:T(128)S(1)} %psum.70), channel_id=1, replica_groups=mesh['grp'=2,'row_0'=8,'row_1'=2,'sub'=8] {'sub'}, use_global_device_ids=true, to_apply=%region_11.12 | all-reduce | flops 2 | bytes 16 | tf_op jit(solution)/shard_map/psum | solution.py:45
  186.9 0.8 multiply_add_fusion.2
  (41 shorter events, 0.5 us)
Async XLA Ops:
  2.4 0.7 copy-start.9
  2.4 0.7 copy-start.11
  3.8 28.1 %copy-start.5 = (f32[4096,32]{0,1:T(8,128)S(1)}, f32[4096,32]{0,1:T(8,128)}, u32[]{:S(2)}) copy-start(f32[4096,32]{0,1:T(8,128)} %param.6) | copy-start | bytes 1572868
  5.2 39.7 %all-to-all-start.1 = ((f32[128,1,512]{2,1,0:T(1,128)}), f32[128,1,512]{2,1,0:T(1,128)S(1)}, u32[]{:S(2)}, u32[]{:S(2)}) async-start(f32[128,1,512]{2,1,0:T(1,128)} %reshape.538), calls=%async_computation.1 | async-start | bytes 524288 | tf_op jit(solution)/shard_map/all_to_all | solution.py:40
  44.9 21.6 %all-to-all-start = ((f32[128,1,512]{2,1,0:T(1,128)}), f32[128,1,512]{2,1,0:T(1,128)S(1)}, u32[]{:S(2)}, u32[]{:S(2)}) async-start(f32[128,1,512]{2,1,0:T(1,128)} %reshape.540), calls=%async_computation | async-start | bytes 524288 | tf_op jit(solution)/shard_map/all_to_all | solution.py:40
  69.1 0.9 copy-start.10
  69.1 0.9 copy-start.12
  69.1 1.9 %copy-start.13 = (f32[32,128]{1,0:T(8,128)S(1)}, f32[32,128]{1,0:T(8,128)}, u32[]{:S(2)}) copy-start(f32[32,128]{1,0:T(8,128)} %get-tuple-element.35) | copy-start | bytes 49156
  69.2 1.9 %copy-start.14 = (f32[32,128]{1,0:T(8,128)S(1)}, f32[32,128]{1,0:T(8,128)}, u32[]{:S(2)}) copy-start(f32[32,128]{1,0:T(8,128)} %get-tuple-element.36) | copy-start | bytes 49156
  71.1 1.0 copy-start.1
  71.3 2.6 %copy-start.2 = (f32[128,1,2,128]{3,0,2,1:T(8,128)S(1)}, f32[128,1,2,128]{3,0,2,1:T(8,128)}, u32[]{:S(2)}) copy-start(f32[128,1,2,128]{3,0,2,1:T(8,128)} %get-tuple-element.22) | copy-start | bytes 393220
  72.1 2.7 %copy-start.6 = (f32[128,32]{0,1:T(8,128)S(1)}, f32[128,32]{0,1:T(8,128)}, u32[]{:S(2)}) copy-start(f32[128,32]{0,1:T(8,128)} %fusion.52) | copy-start | bytes 49156
  74.9 0.7 copy-start.7
  74.9 0.7 copy-start.8
  77.5 20.1 %copy-start.3 = (f32[2,16,2048]{2,1,0:T(8,128)S(1)}, f32[2,16,2048]{2,1,0:T(8,128)}, u32[]{:S(2)}) copy-start(f32[2,16,2048]{2,1,0:T(8,128)} %param.4) | copy-start | bytes 786436
  88.6 26.3 %all-to-all-start.2 = ((f32[128,1,1024]{2,1,0:T(1,128)}), f32[128,1,1024]{2,1,0:T(1,128)S(1)}, u32[]{:S(2)}, u32[]{:S(2)}) async-start(f32[128,1,1024]{2,1,0:T(1,128)} %reshape.542), calls=%async_computation.2 | async-start | bytes 1048576 | tf_op jit(solution)/shard_map/all_to_all | solution.py:111
  118.6 1.2 copy-start
  154.7 33.0 %copy-start.15 = (f32[2]{0:T(128)}, f32[2]{0:T(128)S(1)}, u32[]{:S(2)}) copy-start(f32[2]{0:T(128)S(1)} %div.6) | copy-start | bytes 28
  154.9 32.8 %copy-start.4 = (f32[2,16,2048]{2,1,0:T(8,128)}, f32[2,16,2048]{2,1,0:T(8,128)S(1)}, u32[]{:S(2)}) copy-start(f32[2,16,2048]{2,1,0:T(8,128)S(1)} %get-tuple-element.10) | copy-start | bytes 786436
where the time goes:
time: 188 us
  blocking collectives  66.8 us (36%)
  starting transfers between devices  43.6 us (23%)
  waiting for transfers between devices  34.5 us (18%)
  other arithmetic  20.1 us (11%)
  local copies, waits for them, and re-layouts  13.8 us (7%)
  matrix products  7.18 us (4%)
    psum x6, blocking collectives, over_axes(): return functools.reduce(lax.psum, axes, value)  66.8 us
    all_to_all x2, starting transfers between devices, exchange_in_pieces(): lax.all_to_all(share, axis, split_axis=0, concat_axis=0, tiled=True)  35.2 us
    all_to_all x2, waiting for transfers between devices, exchange_in_pieces(): lax.all_to_all(share, axis, split_axis=0, concat_axis=0, tiled=True)  17.3 us
    all_to_all x1, waiting for transfers between devices, body(): lax.all_to_all(grid_cols, ROW_SUB, split_axis=1, concat_axis=2, tiled=True)  17.1 us
    unnamed x1, other arithmetic  9.61 us
    all_to_all x1, starting transfers between devices, body(): lax.all_to_all(grid_cols, ROW_SUB, split_axis=1, concat_axis=2, tiled=True)  8.38 us
    unnamed x39, local copies, waits for them, and re-layouts  7.4 us
    dot_general x8, matrix products, contract(): jnp.einsum(form_spec, operand, table_arr, precision=lax.Precision.HIGHEST)  7.18 us
  transfers between devices with their start and end apart: 3, of which 3 were waited for; matrix products, arithmetic and copies ran while one was open for 5% of the time, Pallas kernels for 0%

commit v1 on v0

--- a/solution.py
+++ b/solution.py
@@ -10,6 +10,21 @@
 ROW_SUB = ("row_0", "row_1", "sub")
 high_factor = 128
 tiny_value = 1e-06
+
+
+def _arrange_words(load, d_out, k_dim):
+    return jnp.concatenate(
+        lax.all_to_all(
+            jnp.stack(jnp.split(load, lax.psum(1, ROW_SUB), axis=d_out)),
+            ROW_SUB,
+            split_axis=0,
+            concat_axis=0,
+        ),
+        axis=k_dim,
+    )
+
+
+begin_patches = functools.partial(_arrange_words, d_out=1, k_dim=2)
 
 
 def split_up(value, dim, count):
@@ -108,7 +123,7 @@
     inverted = rotate(inverted, turn_cos[:, :, None, None], -turn_sin[:, :, None, None], 4)
     grid_cols = contract("fbjqcm,jcda->fabqdm", inverted, complex_table(last_cos, last_sin))
     grid_cols = grid_cols.reshape(batches, grid_len, 2 * embed_len // devices)
-    rows_back = lax.all_to_all(grid_cols, ROW_SUB, split_axis=1, concat_axis=2, tiled=True)
+    rows_back = begin_patches(grid_cols)
     rows_back = rows_back.reshape(batches, rows_dev, high_factor, 2, low_factor)
     mixed = contract("frkcm,kcdb->frbdm", rows_back, complex_table(perm_cos, perm_sin))
     mixed = rotate(mixed, turn_cos, -turn_sin, 3)

time: 188 us -> 294 us (1.56); the launches traced: 188 us -> 288 us
  local copies, waits for them, and re-layouts: 13.8 us -> 122 us
  other arithmetic: 20.1 us -> 9.86 us
    unnamed x39 -> x376, local copies, waits for them, and re-layouts: 7.4 us -> 112 us
    unnamed x1 -> x0, other arithmetic: 9.61 us -> none
    split x0 -> x7, local copies, waits for them, and re-layouts: none -> 4.47 us  [_arrange_words(): jnp.split(load, lax.psum(1, ROW_SUB), axis=d_out)]
  transfers between devices with their start and end apart: 3 -> 3, of which waited for: 3 -> 3; matrix products, arithmetic and copies ran while one was open for 5% -> 3% of each run, Pallas kernels for 0% -> 0%
where the time goes in v1:
time: 294 us; the launch traced here: 288 us
  local copies, waits for them, and re-layouts  122 us (41%)
  blocking collectives  66.8 us (23%)
  starting transfers between devices  43.6 us (15%)
  waiting for transfers between devices  35.1 us (12%)
  other arithmetic  9.86 us (3%)
  matrix products  7.18 us (2%)
  between operations  3.38 us (1%)
    unnamed x376, local copies, waits for them, and re-layouts  112 us
    psum x6, blocking collectives, over_axes(): return functools.reduce(lax.psum, axes, value)  66.8 us
    all_to_all x2, starting transfers between devices, exchange_in_pieces(): lax.all_to_all(share, axis, split_axis=0, concat_axis=0, tiled=True)  35.2 us
    all_to_all x2, waiting for transfers between devices, exchange_in_pieces(): lax.all_to_all(share, axis, split_axis=0, concat_axis=0, tiled=True)  18 us
    all_to_all x1, waiting for transfers between devices, _arrange_words(): lax.all_to_all(jnp.stack(jnp.split(load, lax.psum(1, ROW_SUB), axis=d_out...  17.1 us
    all_to_all x1, starting transfers between devices, _arrange_words(): lax.all_to_all(jnp.stack(jnp.split(load, lax.psum(1, ROW_SUB), axis=d_out...  8.35 us
    dot_general x8, matrix products, contract(): jnp.einsum(form_spec, operand, table_arr, precision=lax.Precision.HIGHEST)  7.18 us
  transfers between devices with their start and end apart: 3, of which 3 were waited for; matrix products, arithmetic and copies ran while one was open for 3% of the time, Pallas kernels for 0%

profile of v1, /device:TPU:514, one launch (start us, length us, event | category | flops | bytes accessed | tf_op | source)
XLA Modules:
  0.0 288.1 jit_solution(4940952107176007568)
XLA Ops:
  5.8 26.7 %all-to-all-start.1 = ((f32[128,1,512]{2,1,0:T(1,128)}), f32[128,1,512]{2,1,0:T(1,128)S(1)}, u32[]{:S(2)}, u32[]{:S(2)}) async-start(f32[128,1,512]{2,1,0:T(1,128)} %reshape.540), calls=%async_computation.1 | async-start | bytes 524288 | tf_op jit(solution)/shard_map/all_to_all | solution.py:55
  34.5 1.5 copy.466
  37.4 8.1 %all-to-all-done.1 = f32[128,1,512]{2,1,0:T(1,128)S(1)} async-done(((f32[128,1,512]{2,1,0:T(1,128)}), f32[128,1,512]{2,1,0:T(1,128)S(1)}, u32[]{:S(2)}, u32[]{:S(2)}) %all-to-all-start.1) | async-done | bytes 262176 | tf_op jit(solution)/shard_map/all_to_all | solution.py:55
  45.5 8.5 %all-to-all-start = ((f32[128,1,512]{2,1,0:T(1,128)}), f32[128,1,512]{2,1,0:T(1,128)S(1)}, u32[]{:S(2)}, u32[]{:S(2)}) async-start(f32[128,1,512]{2,1,0:T(1,128)} %reshape.542), calls=%async_computation | async-start | bytes 524288 | tf_op jit(solution)/shard_map/all_to_all | solution.py:55
  57.2 9.9 %all-to-all-done = f32[128,1,512]{2,1,0:T(1,128)S(1)} async-done(((f32[128,1,512]{2,1,0:T(1,128)}), f32[128,1,512]{2,1,0:T(1,128)S(1)}, u32[]{:S(2)}, u32[]{:S(2)}) %all-to-all-start) | async-done | bytes 262176 | tf_op jit(solution)/shard_map/all_to_all | solution.py:55
  72.8 1.7 fusion.1
  82.1 1.4 copy.619
  83.6 1.4 copy.620
  86.4 1.4 copy.622
  87.8 1.4 copy.623
  89.3 1.4 copy.624
  90.7 1.4 copy.625
  92.1 1.4 copy.626
  93.5 1.4 copy.627
  96.4 1.4 copy.629
  97.8 1.4 copy.630
  99.2 1.4 copy.631
  100.6 1.4 copy.632
  103.5 1.4 copy.634
  106.3 1.4 copy.636
  107.7 1.4 copy.637
  109.2 1.4 copy.638
  110.6 1.4 copy.639
  112.0 1.4 copy.640
  113.4 1.4 copy.641
  114.9 1.4 copy.642
  116.3 1.4 copy.643
  117.7 1.4 copy.644
  119.1 1.4 copy.645
  122.0 1.4 copy.647
  123.4 1.4 copy.648
  124.8 1.4 copy.649
  126.2 1.4 copy.650
  127.6 1.4 copy.651
  129.1 1.4 copy.652
  130.5 1.4 copy.653
  131.9 1.4 copy.654
  133.3 1.4 copy.655
  134.8 1.4 copy.656
  136.2 1.4 copy.657
  137.6 1.4 copy.658
  141.9 1.4 copy.661
  144.7 1.4 copy.663
  146.1 1.4 copy.664
  147.6 1.4 copy.665
  149.0 1.4 copy.666
  150.4 1.4 copy.667
  153.2 1.4 copy.669
  154.7 1.4 copy.670
  156.1 1.4 copy.671
  158.9 1.4 copy.673
  160.4 1.4 copy.674
  161.8 1.4 copy.675
  166.0 1.4 copy.678
  188.6 1.4 reshape.544
  190.1 8.4 %all-to-all-start.2 = ((f32[128,1,1024]{2,1,0:T(1,128)}), f32[128,1,1024]{2,1,0:T(1,128)S(1)}, u32[]{:S(2)}, u32[]{:S(2)}) async-start(f32[128,1,1024]{2,1,0:T(1,128)} %reshape.544), calls=%async_computation.2 | async-start | bytes 1048576 | tf_op jit(solution)/shard_map/all_to_all | solution.py:17
  199.2 17.1 %all-to-all-done.2 = f32[128,1,1024]{2,1,0:T(1,128)S(1)} async-done(((f32[128,1,1024]{2,1,0:T(1,128)}), f32[128,1,1024]{2,1,0:T(1,128)S(1)}, u32[]{:S(2)}, u32[]{:S(2)}) %all-to-all-start.2) | async-done | bytes 524320 | tf_op jit(solution)/shard_map/all_to_all | solution.py:17
  216.4 1.9 reduce.2
  220.3 15.7 %all-reduce.1 = (f32[2]{0:T(128)S(1)}, f32[2]{0:T(128)S(1)}) all-reduce(f32[2]{0:T(128)S(1)} %multiply_reduce_fusion.2, f32[2]{0:T(128)S(1)} %multiply_reduce_fusion.1), channel_id=1, replica_groups=mesh['grp'=2,'row_0'=8,'row_1'=2,'sub'=8] {'row_0'}, use_global_device_ids=true, to_apply=%region_1.2 | all-reduce | flops 4 | bytes 32 | tf_op jit(solution)/shard_map/psum | solution.py:60
  236.0 2.5 all-reduce.2
  238.5 16.5 %all-reduce = (f32[2]{0:T(128)S(1)}, f32[2]{0:T(128)S(1)}) all-reduce(f32[2]{0:T(128)S(1)} %get-tuple-element.7, f32[2]{0:T(128)S(1)} %get-tuple-element.8), channel_id=1, replica_groups=mesh['grp'=2,'row_0'=8,'row_1'=2,'sub'=8] {'sub'}, use_global_device_ids=true, to_apply=%region_3.4 | all-reduce | flops 4 | bytes 32 | tf_op jit(solution)/shard_map/psum | solution.py:60
  255.3 15.3 %psum.69 = f32[2]{0:T(128)S(1)} all-reduce(f32[2]{0:T(128)S(1)} %get-tuple-element.9), channel_id=1, replica_groups=mesh['grp'=2,'row_0'=8,'row_1'=2,'sub'=8] {'row_0'}, use_global_device_ids=true, to_apply=%region_9.10 | all-reduce | flops 2 | bytes 16 | tf_op jit(solution)/shard_map/psum | solution.py:60
  270.6 2.5 psum.70
  273.1 14.2 %psum.71 = f32[2]{0:T(128)S(1)} all-reduce(f32[2]{0:T(128)S(1)} %psum.70), channel_id=1, replica_groups=mesh['grp'=2,'row_0'=8,'row_1'=2,'sub'=8] {'sub'}, use_global_device_ids=true, to_apply=%region_11.12 | all-reduce | flops 2 | bytes 16 | tf_op jit(solution)/shard_map/psum | solution.py:60
  (384 shorter events, 64.5 us)
Async XLA Ops:
  2.4 0.7 copy-start.10
  2.4 0.7 copy-start.12
  3.2 0.7 copy-start.2
  4.4 28.1 %copy-start.6 = (f32[4096,32]{0,1:T(8,128)S(1)}, f32[4096,32]{0,1:T(8,128)}, u32[]{:S(2)}) copy-start(f32[4096,32]{0,1:T(8,128)} %param.6) | copy-start | bytes 1572868
  5.8 39.7 %all-to-all-start.1 = ((f32[128,1,512]{2,1,0:T(1,128)}), f32[128,1,512]{2,1,0:T(1,128)S(1)}, u32[]{:S(2)}, u32[]{:S(2)}) async-start(f32[128,1,512]{2,1,0:T(1,128)} %reshape.540), calls=%async_computation.1 | async-start | bytes 524288 | tf_op jit(solution)/shard_map/all_to_all | solution.py:55
  45.5 21.6 %all-to-all-start = ((f32[128,1,512]{2,1,0:T(1,128)}), f32[128,1,512]{2,1,0:T(1,128)S(1)}, u32[]{:S(2)}, u32[]{:S(2)}) async-start(f32[128,1,512]{2,1,0:T(1,128)} %reshape.542), calls=%async_computation | async-start | bytes 524288 | tf_op jit(solution)/shard_map/all_to_all | solution.py:55
  69.8 0.9 copy-start.11
  69.8 0.9 copy-start.13
  69.8 1.9 copy-start.14
  69.8 1.9 copy-start.15
  71.8 1.0 copy-start.1
  71.8 1.1 copy-start.3
  72.8 2.7 copy-start.7
  75.5 0.7 copy-start.8
  75.5 0.7 copy-start.9
  168.3 19.5 %copy-start.18 = (f32[1,16,64]{2,1,0:T(8,128)S(1)}, f32[1,16,64]{2,1,0:T(8,128)}, u32[]{:S(2)}) copy-start(f32[1,16,64]{2,1,0:T(8,128)} %copy.676) | copy-start | bytes 12292
  168.3 19.5 %copy-start.17 = (f32[1,16,64]{2,1,0:T(8,128)S(1)}, f32[1,16,64]{2,1,0:T(8,128)}, u32[]{:S(2)}) copy-start(f32[1,16,64]{2,1,0:T(8,128)} %copy.677) | copy-start | bytes 12292
  168.3 19.5 %copy-start.16 = (f32[1,16,64]{2,1,0:T(8,128)S(1)}, f32[1,16,64]{2,1,0:T(8,128)}, u32[]{:S(2)}) copy-start(f32[1,16,64]{2,1,0:T(8,128)} %copy.678) | copy-start | bytes 12292
  168.4 19.3 %copy-start.21 = (f32[1,16,64]{2,1,0:T(8,128)S(1)}, f32[1,16,64]{2,1,0:T(8,128)}, u32[]{:S(2)}) copy-start(f32[1,16,64]{2,1,0:T(8,128)} %copy.673) | copy-start | bytes 12292
  168.4 19.4 %copy-start.20 = (f32[1,16,64]{2,1,0:T(8,128)S(1)}, f32[1,16,64]{2,1,0:T(8,128)}, u32[]{:S(2)}) copy-start(f32[1,16,64]{2,1,0:T(8,128)} %copy.674) | copy-start | bytes 12292
  168.4 19.4 %copy-start.19 = (f32[1,16,64]{2,1,0:T(8,128)S(1)}, f32[1,16,64]{2,1,0:T(8,128)}, u32[]{:S(2)}) copy-start(f32[1,16,64]{2,1,0:T(8,128)} %copy.675) | copy-start | bytes 12292
  168.5 19.2 %copy-start.24 = (f32[1,16,64]{2,1,0:T(8,128)S(1)}, f32[1,16,64]{2,1,0:T(8,128)}, u32[]{:S(2)}) copy-start(f32[1,16,64]{2,1,0:T(8,128)} %copy.670) | copy-start | bytes 12292
  168.5 19.2 %copy-start.23 = (f32[1,16,64]{2,1,0:T(8,128)S(1)}, f32[1,16,64]{2,1,0:T(8,128)}, u32[]{:S(2)}) copy-start(f32[1,16,64]{2,1,0:T(8,128)} %copy.671) | copy-start | bytes 12292
  168.5 19.2 %copy-start.22 = (f32[1,16,64]{2,1,0:T(8,128)S(1)}, f32[1,16,64]{2,1,0:T(8,128)}, u32[]{:S(2)}) copy-start(f32[1,16,64]{2,1,0:T(8,128)} %copy.672) | copy-start | bytes 12292
  168.6 19.1 %copy-start.27 = (f32[1,16,64]{2,1,0:T(8,128)S(1)}, f32[1,16,64]{2,1,0:T(8,128)}, u32[]{:S(2)}) copy-start(f32[1,16,64]{2,1,0:T(8,128)} %copy.667) | copy-start | bytes 12292
  168.6 19.1 %copy-start.25 = (f32[1,16,64]{2,1,0:T(8,128)S(1)}, f32[1,16,64]{2,1,0:T(8,128)}, u32[]{:S(2)}) copy-start(f32[1,16,64]{2,1,0:T(8,128)} %copy.668) | copy-start | bytes 12292
  168.6 19.1 %copy-start.26 = (f32[1,16,64]{2,1,0:T(8,128)S(1)}, f32[1,16,64]{2,1,0:T(8,128)}, u32[]{:S(2)}) copy-start(f32[1,16,64]{2,1,0:T(8,128)} %copy.669) | copy-start | bytes 12292
  168.7 18.9 %copy-start.30 = (f32[1,16,64]{2,1,0:T(8,128)S(1)}, f32[1,16,64]{2,1,0:T(8,128)}, u32[]{:S(2)}) copy-start(f32[1,16,64]{2,1,0:T(8,128)} %copy.664) | copy-start | bytes 12292
  168.7 18.9 %copy-start.29 = (f32[1,16,64]{2,1,0:T(8,128)S(1)}, f32[1,16,64]{2,1,0:T(8,128)}, u32[]{:S(2)}) copy-start(f32[1,16,64]{2,1,0:T(8,128)} %copy.665) | copy-start | bytes 12292
  168.7 18.9 %copy-start.28 = (f32[1,16,64]{2,1,0:T(8,128)S(1)}, f32[1,16,64]{2,1,0:T(8,128)}, u32[]{:S(2)}) copy-start(f32[1,16,64]{2,1,0:T(8,128)} %copy.666) | copy-start | bytes 12292
  168.7 18.8 %copy-start.33 = (f32[1,16,64]{2,1,0:T(8,128)S(1)}, f32[1,16,64]{2,1,0:T(8,128)}, u32[]{:S(2)}) copy-start(f32[1,16,64]{2,1,0:T(8,128)} %copy.661) | copy-start | bytes 12292
  168.7 18.8 %copy-start.32 = (f32[1,16,64]{2,1,0:T(8,128)S(1)}, f32[1,16,64]{2,1,0:T(8,128)}, u32[]{:S(2)}) copy-start(f32[1,16,64]{2,1,0:T(8,128)} %copy.662) | copy-start | bytes 12292
  168.7 18.8 %copy-start.31 = (f32[1,16,64]{2,1,0:T(8,128)S(1)}, f32[1,16,64]{2,1,0:T(8,128)}, u32[]{:S(2)}) copy-start(f32[1,16,64]{2,1,0:T(8,128)} %copy.663) | copy-start | bytes 12292
  168.8 18.6 %copy-start.36 = (f32[1,16,64]{2,1,0:T(8,128)S(1)}, f32[1,16,64]{2,1,0:T(8,128)}, u32[]{:S(2)}) copy-start(f32[1,16,64]{2,1,0:T(8,128)} %copy.658) | copy-start | bytes 12292
  168.8 18.6 %copy-start.35 = (f32[1,16,64]{2,1,0:T(8,128)S(1)}, f32[1,16,64]{2,1,0:T(8,128)}, u32[]{:S(2)}) copy-start(f32[1,16,64]{2,1,0:T(8,128)} %copy.659) | copy-start | bytes 12292
  168.8 18.7 %copy-start.34 = (f32[1,16,64]{2,1,0:T(8,128)S(1)}, f32[1,16,64]{2,1,0:T(8,128)}, u32[]{:S(2)}) copy-start(f32[1,16,64]{2,1,0:T(8,128)} %copy.660) | copy-start | bytes 12292
  168.9 18.5 %copy-start.39 = (f32[1,16,64]{2,1,0:T(8,128)S(1)}, f32[1,16,64]{2,1,0:T(8,128)}, u32[]{:S(2)}) copy-start(f32[1,16,64]{2,1,0:T(8,128)} %copy.655) | copy-start | bytes 12292
  168.9 18.5 %copy-start.38 = (f32[1,16,64]{2,1,0:T(8,128)S(1)}, f32[1,16,64]{2,1,0:T(8,128)}, u32[]{:S(2)}) copy-start(f32[1,16,64]{2,1,0:T(8,128)} %copy.656) | copy-start | bytes 12292
  168.9 18.5 %copy-start.37 = (f32[1,16,64]{2,1,0:T(8,128)S(1)}, f32[1,16,64]{2,1,0:T(8,128)}, u32[]{:S(2)}) copy-start(f32[1,16,64]{2,1,0:T(8,128)} %copy.657) | copy-start | bytes 12292
  169.0 18.3 %copy-start.42 = (f32[1,16,64]{2,1,0:T(8,128)S(1)}, f32[1,16,64]{2,1,0:T(8,128)}, u32[]{:S(2)}) copy-start(f32[1,16,64]{2,1,0:T(8,128)} %copy.652) | copy-start | bytes 12292
  169.0 18.4 %copy-start.41 = (f32[1,16,64]{2,1,0:T(8,128)S(1)}, f32[1,16,64]{2,1,0:T(8,128)}, u32[]{:S(2)}) copy-start(f32[1,16,64]{2,1,0:T(8,128)} %copy.653) | copy-start | bytes 12292
  169.0 18.4 %copy-start.40 = (f32[1,16,64]{2,1,0:T(8,128)S(1)}, f32[1,16,64]{2,1,0:T(8,128)}, u32[]{:S(2)}) copy-start(f32[1,16,64]{2,1,0:T(8,128)} %copy.654) | copy-start | bytes 12292
  169.0 18.2 %copy-start.44 = (f32[1,16,64]{2,1,0:T(8,128)S(1)}, f32[1,16,64]{2,1,0:T(8,128)}, u32[]{:S(2)}) copy-start(f32[1,16,64]{2,1,0:T(8,128)} %copy.649) | copy-start | bytes 12292
  169.0 18.2 %copy-start.45 = (f32[1,16,64]{2,1,0:T(8,128)S(1)}, f32[1,16,64]{2,1,0:T(8,128)}, u32[]{:S(2)}) copy-start(f32[1,16,64]{2,1,0:T(8,128)} %copy.650) | copy-start | bytes 12292
  169.1 18.2 %copy-start.43 = (f32[1,16,64]{2,1,0:T(8,128)S(1)}, f32[1,16,64]{2,1,0:T(8,128)}, u32[]{:S(2)}) copy-start(f32[1,16,64]{2,1,0:T(8,128)} %copy.651) | copy-start | bytes 12292
  169.1 18.1 %copy-start.48 = (f32[1,16,64]{2,1,0:T(8,128)S(1)}, f32[1,16,64]{2,1,0:T(8,128)}, u32[]{:S(2)}) copy-start(f32[1,16,64]{2,1,0:T(8,128)} %copy.646) | copy-start | bytes 12292
  169.1 18.1 %copy-start.47 = (f32[1,16,64]{2,1,0:T(8,128)S(1)}, f32[1,16,64]{2,1,0:T(8,128)}, u32[]{:S(2)}) copy-start(f32[1,16,64]{2,1,0:T(8,128)} %copy.647) | copy-start | bytes 12292
  169.1 18.1 %copy-start.46 = (f32[1,16,64]{2,1,0:T(8,128)S(1)}, f32[1,16,64]{2,1,0:T(8,128)}, u32[]{:S(2)}) copy-start(f32[1,16,64]{2,1,0:T(8,128)} %copy.648) | copy-start | bytes 12292
  169.2 17.9 %copy-start.51 = (f32[1,16,64]{2,1,0:T(8,128)S(1)}, f32[1,16,64]{2,1,0:T(8,128)}, u32[]{:S(2)}) copy-start(f32[1,16,64]{2,1,0:T(8,128)} %copy.643) | copy-start | bytes 12292
  169.2 17.9 %copy-start.50 = (f32[1,16,64]{2,1,0:T(8,128)S(1)}, f32[1,16,64]{2,1,0:T(8,128)}, u32[]{:S(2)}) copy-start(f32[1,16,64]{2,1,0:T(8,128)} %copy.644) | copy-start | bytes 12292
  169.2 17.9 %copy-start.49 = (f32[1,16,64]{2,1,0:T(8,128)S(1)}, f32[1,16,64]{2,1,0:T(8,128)}, u32[]{:S(2)}) copy-start(f32[1,16,64]{2,1,0:T(8,128)} %copy.645) | copy-start | bytes 12292
  169.3 17.8 %copy-start.54 = (f32[1,16,64]{2,1,0:T(8,128)S(1)}, f32[1,16,64]{2,1,0:T(8,128)}, u32[]{:S(2)}) copy-start(f32[1,16,64]{2,1,0:T(8,128)} %copy.640) | copy-start | bytes 12292
  169.3 17.8 %copy-start.53 = (f32[1,16,64]{2,1,0:T(8,128)S(1)}, f32[1,16,64]{2,1,0:T(8,128)}, u32[]{:S(2)}) copy-start(f32[1,16,64]{2,1,0:T(8,128)} %copy.641) | copy-start | bytes 12292
  169.3 17.8 %copy-start.52 = (f32[1,16,64]{2,1,0:T(8,128)S(1)}, f32[1,16,64]{2,1,0:T(8,128)}, u32[]{:S(2)}) copy-start(f32[1,16,64]{2,1,0:T(8,128)} %copy.642) | copy-start | bytes 12292
  169.4 17.7 %copy-start.55 = (f32[1,16,64]{2,1,0:T(8,128)S(1)}, f32[1,16,64]{2,1,0:T(8,128)}, u32[]{:S(2)}) copy-start(f32[1,16,64]{2,1,0:T(8,128)} %copy.639) | copy-start | bytes 12292
  187.3 11.8 %copy-start.4 = (f32[2,16,2048]{2,1,0:T(8,128)S(1)}, f32[2,16,2048]{2,1,0:T(8,128)}, u32[]{:S(2)}) copy-start(f32[2,16,2048]{2,1,0:T(8,128)} %param.4) | copy-start | bytes 786436
  190.1 26.3 %all-to-all-start.2 = ((f32[128,1,1024]{2,1,0:T(1,128)}), f32[128,1,1024]{2,1,0:T(1,128)S(1)}, u32[]{:S(2)}, u32[]{:S(2)}) async-start(f32[128,1,1024]{2,1,0:T(1,128)} %reshape.544), calls=%async_computation.2 | async-start | bytes 1048576 | tf_op jit(solution)/shard_map/all_to_all | solution.py:17
  219.0 1.2 copy-start
  255.1 33.0 %copy-start.56 = (f32[2]{0:T(128)}, f32[2]{0:T(128)S(1)}, u32[]{:S(2)}) copy-start(f32[2]{0:T(128)S(1)} %div.6) | copy-start | bytes 28
  255.3 32.8 %copy-start.5 = (f32[2,16,2048]{2,1,0:T(8,128)}, f32[2,16,2048]{2,1,0:T(8,128)S(1)}, u32[]{:S(2)}) copy-start(f32[2,16,2048]{2,1,0:T(8,128)S(1)} %get-tuple-element.10) | copy-start | bytes 786436
